TPU v7x, 32 devices: a whole 2x2x4 slice. The times are simulated.
32 devices in a mesh: grp: 4 (over y, x), zero: 8 (over z, core).
Axes of the slice: x: 2, y: 2, z: 4, core: 2. Of those that a mesh axis runs over, the one named last changes fastest.
Arguments:
- replica_grads: bfloat16 [4, 3072, 2, 12288], P('grp', None, None, 'zero'), may hold values from -20000 to 20000, as said below
- master_weights: float32 [3072, 2, 12288], P(('grp', 'zero')), may hold values from -0.6 to 0.6
- first_moment: float32 [3072, 2, 12288], P(('grp', 'zero')), may hold values from -0.3 to 0.3
- second_moment: float32 [3072, 2, 12288], P(('grp', 'zero')), may hold values from 0.001 to 0.03
- max_norm: float32 [1], replicated, may hold values from 1737.7856 to 4344.464
Outputs:
- new_master: float32 [3072, 2, 12288], P(('grp', 'zero'))
- new_first: float32 [3072, 2, 12288], P(('grp', 'zero'))
- new_second: float32 [3072, 2, 12288], P(('grp', 'zero'))
- new_weights: bfloat16 [3072, 2, 12288], P(None, None, 'zero')
Inputs may be any that keep to these rules, and one draw needn't show every extreme that they name: `replica_grads`: one gradient of the joined weight for each replica group.
All inputs are finite; a program needn't handle non-finite values.
Results may differ from a plain program's by a relative error of at most 0.015.
Values may be sent and summed in bfloat16 or wider, within the bound.
A program may use at most 192 MiB of HBM per device.

v0:
```python
import jax
import jax.numpy as jnp
from jax import lax
from jax.sharding import PartitionSpec as P

ADAM_STEP = 10
beta_one = 0.9
beta_two = 0.95
learn_rate = 0.02
adam_eps = 1e-08
norm_eps = 1e-06


def adam_update(summed, master, first, second, scale):
    clipped = summed * scale
    new_first = beta_one * first + (1.0 - beta_one) * clipped
    new_second = beta_two * second + (1.0 - beta_two) * clipped * clipped
    correct_one = 1.0 - beta_one**ADAM_STEP
    correct_two = 1.0 - beta_two**ADAM_STEP
    step_size = new_first / correct_one / (jnp.sqrt(new_second / correct_two) + adam_eps)
    new_master = master - learn_rate * step_size
    return (new_master, new_first, new_second)


def body(replica_grads, master_weights, first_moment, second_moment, max_norm):
    groups = lax.axis_size("grp")
    shards = lax.axis_size("zero")
    local_grad = replica_grads[0]
    local_width = local_grad.shape[2]
    rows_dev = master_weights.shape[0]
    full_width = master_weights.shape[2]
    blocks = local_grad.reshape(groups, shards, rows_dev, 2, local_width)
    arrived = lax.all_to_all(
        lax.all_to_all(blocks[None], "grp", split_axis=1, concat_axis=0, tiled=True),
        "zero",
        split_axis=2,
        concat_axis=5,
        tiled=True,
    )
    summed = jnp.sum(arrived.astype(jnp.float32), axis=0)
    summed = summed.reshape(master_weights.shape)
    total = lax.psum(jnp.sum(summed * summed), ("grp", "zero"))
    scale = jnp.minimum(jnp.float32(1.0), max_norm[0] / (jnp.sqrt(total) + norm_eps))
    new_master, new_first, new_second = adam_update(
        summed, master_weights, first_moment, second_moment, scale
    )
    fresh = new_master.astype(jnp.bfloat16).reshape(1, 1, rows_dev, 2, full_width)
    own_tiles = lax.all_to_all(fresh, "zero", split_axis=4, concat_axis=1, tiled=True)
    tiled = lax.all_gather(own_tiles, "grp", axis=0, tiled=True)
    new_weights = tiled.reshape(groups * shards * rows_dev, 2, full_width // shards)
    return (new_master, new_first, new_second, new_weights)


def solution(mesh):
    in_specs = (
        P("grp", None, None, "zero"),
        P(("grp", "zero"), None, None),
        P(("grp", "zero"), None, None),
        P(("grp", "zero"), None, None),
        P(),
    )
    out_specs = (
        P(("grp", "zero"), None, None),
        P(("grp", "zero"), None, None),
        P(("grp", "zero"), None, None),
        P(None, None, "zero"),
    )
    return jax.shard_map(body, mesh=mesh, in_specs=in_specs, out_specs=out_specs, check_vma=False)
```

profile of v0, /device:TPU:0, one launch (start us, length us, event | category | flops | bytes accessed | tf_op | source)
XLA Modules:
  0.0 1264.3 jit_solution(17715620397299692491)
XLA Ops:
  7.2 0.0 all-gather.3.cloned.1.call-start
  7.2 218.8 %all_to_all.39 = bf16[1,4,8,96,2,1536]{5,4,3,2,0,1:T(2,128)(2,1)} all-to-all(bf16[1,4,8,96,2,1536]{5,4,3,2,0,1:T(2,128)(2,1)} %bitcast.20), channel_id=1, replica_groups=mesh['grp'=4,'zero'=8] {'grp'}, dimensions={1} | all-to-all | bytes 37748736 | tf_op jit(solution)/shard_map/all_to_all | solution.py:34
  226.0 15.4 %copy.48 = bf16[4,1,8,96,2,1536]{5,4,3,0,1,2:T(2,128)(2,1)S(1)} copy(bf16[4,1,8,96,2,1536]{5,4,3,2,0,1:T(2,128)(2,1)} %bitcast.16) | data formatting | bytes 37748736 | tf_op jit(solution)/shard_map/all_to_all | solution.py:34
  241.4 413.5 %all_to_all.40 = bf16[4,1,8,96,2,1536]{5,4,3,0,1,2:T(2,128)(2,1)} all-to-all(bf16[4,1,8,96,2,1536]{5,4,3,0,1,2:T(2,128)(2,1)S(1)} %copy.48), channel_id=1, replica_groups=mesh['grp'=4,'zero'=8] {'zero'}, dimensions={2} | all-to-all | bytes 37748736 | tf_op jit(solution)/shard_map/all_to_all | solution.py:33
  654.9 17.5 %convert_reduce_fusion = f32[8,96,2,1536]{3,1,2,0:T(8,128)} fusion(bf16[4,1,8,96,2,1536]{5,4,3,0,1,2:T(2,128)(2,1)} %all_to_all.40), kind=kLoop, calls=%fused_computation | loop fusion | flops 16515072 | bytes 28311552 | tf_op jit(solution)/shard_map/reduce_sum | solution.py:40
  672.5 14.0 %multiply_reduce_fusion = f32[]{:T(128)} fusion(f32[8,96,2,1536]{3,1,2,0:T(8,128)} %convert_reduce_fusion), kind=kLoop, calls=%fused_computation.8 | loop fusion | flops 4718591 | bytes 9437188 | tf_op jit(solution)/shard_map/reduce_sum | solution.py:42
  687.1 38.2 %psum.7 = f32[]{:T(128)} all-reduce(f32[]{:T(128)} %multiply_reduce_fusion), channel_id=1, replica_groups=mesh['grp'=4,'zero'=8] {'grp','zero'}, use_global_device_ids=true, to_apply=%region_2.0 | all-reduce | flops 1 | bytes 8 | tf_op jit(solution)/shard_map/psum | solution.py:42
  726.0 16.1 %multiply_bitcast_fusion = f32[96,2,8,1536]{3,1,0,2:T(2,128)S(1)} fusion(f32[8,96,2,1536]{3,1,2,0:T(8,128)} %convert_reduce_fusion, f32[]{:T(128)S(6)} %min_shard_map.3), kind=kLoop, calls=%fused_computation.7 | loop fusion | flops 2359296 | bytes 18874372 | tf_op jit(solution)/shard_map/mul | solution.py:15
  742.1 9.2 copy.51
  751.3 10.0 mul.56
  761.3 33.4 %convert_bitcast_fusion = (bf16[1,1,96,2,12288]{4,2,3,1,0:T(8,128)(2,1)}, f32[96,2,12288]{2,0,1:T(8,128)}, f32[96,2,12288]{2,0,1:T(8,128)}, f32[96,2,12288]{2,0,1:T(8,128)}) fusion(f32[96,2,12288]{2,1,0:T(2,128)} %param.6, f32[96,2,12288]{2,0,1:T(8,128)} %mul.56, f32[96,2,12288]{2,1,0:T(2,128)} %param.7, f32[96,2,12288]{2,1,0:T(2,128)} %param.8), kind=kLoop, calls=%fused_computation.9 | loop fusion | flops 33030144 | bytes 70778880 | tf_op jit(solution)/shard_map/reshape | solution.py:47
  794.7 14.1 %copy.54 = bf16[1,1,96,2,12288]{2,3,1,0,4:T(2,128)(2,1)} copy(bf16[1,1,96,2,12288]{4,2,3,1,0:T(8,128)(2,1)} %get-tuple-element.20) | data formatting | bytes 9437184 | tf_op jit(solution)/shard_map/reshape | solution.py:47
  808.8 144.7 %all_to_all.41 = bf16[1,1,96,2,12288]{2,3,1,0,4:T(2,128)(2,1)} all-to-all(bf16[1,1,96,2,12288]{2,3,1,0,4:T(2,128)(2,1)} %copy.54), channel_id=1, replica_groups=mesh['grp'=4,'zero'=8] {'zero'}, dimensions={4} | all-to-all | bytes 9437184 | tf_op jit(solution)/shard_map/all_to_all | solution.py:48
  953.5 15.8 %copy.55 = bf16[1,1,96,2,8,1536]{5,2,3,1,4,0:T(8,128)(2,1)} copy(bf16[1,1,96,2,8,1536]{2,3,5,4,1,0:T(2,128)(2,1)} %bitcast.19) | data formatting | bytes 9437184 | tf_op jit(solution)/shard_map/all_to_all | solution.py:48
  969.3 0.0 all-gather.3.cloned.1.call-update
  969.3 0.0 slice-start
  969.3 0.0 slice-start.1
  969.3 17.2 %copy.57 = f32[96,2,12288]{2,1,0:T(2,128)} copy(f32[96,2,12288]{2,0,1:T(8,128)} %get-tuple-element.21) | data formatting | bytes 18874368
  986.6 0.0 slice-start.2
  986.6 17.1 %copy.58 = f32[96,2,12288]{2,1,0:T(2,128)} copy(f32[96,2,12288]{2,0,1:T(8,128)} %get-tuple-element.22) | data formatting | bytes 18874368
  1003.7 0.0 slice-done
  1003.7 0.0 slice-done.1
  1003.7 0.0 slice-done.2
  1003.7 16.1 %copy.59 = f32[96,2,12288]{2,1,0:T(2,128)} copy(f32[96,2,12288]{2,0,1:T(8,128)S(1)} %bitcast.18) | data formatting | bytes 18874368
  1019.8 124.6 %all-gather.3.cloned.1.call-done = bf16[4,8,1,96,2,1536]{5,3,4,2,1,0:T(8,128)(2,1)} async-done(((bf16[1,8,1,96,2,1536]{5,3,4,2,1,0:T(8,128)(2,1)}), bf16[4,8,1,96,2,1536]{5,3,4,2,1,0:T(8,128)(2,1)}) %all-gather.3.cloned.1.call-update) | async-done | bytes 18874384 | tf_op jit(solution)/shard_map/all_gather | solution.py:49
  1144.4 9.5 copy.56
  1153.9 103.4 %copy.60 = bf16[3072,2,1536]{2,1,0:T(2,128)(2,1)} copy(bf16[3072,2,1536]{2,0,1:T(8,128)(2,1)S(1)} %bitcast.15) | data formatting | bytes 37748736
  (1 shorter events, 0.0 us)
Async XLA Ops:
  7.2 1137.2 %all-gather.3.cloned.1.call-start = ((), (), s32[]{:S(2)}) async-start(), calls=%async_computation.3 | async-start | bytes 23592960 | tf_op jit(solution)/shard_map/all_gather | solution.py:49
  969.3 34.4 %slice-start = ((s8[9437184]{0:T(1024)(128)(4,1)}), s8[4194304]{0:T(1024)(128)(4,1)S(1)}, s32[]{:S(2)}) async-start(s8[9437184]{0:T(1024)(128)(4,1)} %bitcast.17), calls=%async_computation.4 | async-start | bytes 8388608
  969.3 34.4 %slice-start.1 = ((s8[9437184]{0:T(1024)(128)(4,1)}), s8[4194304]{0:T(1024)(128)(4,1)S(1)}, s32[]{:S(2)}) async-start(s8[9437184]{0:T(1024)(128)(4,1)} %bitcast.17), calls=%async_computation.5 | async-start | bytes 8388608
  986.6 17.2 %slice-start.2 = ((s8[9437184]{0:T(1024)(128)(4,1)}), s8[1048576]{0:T(1024)(128)(4,1)S(1)}, s32[]{:S(2)}) async-start(s8[9437184]{0:T(1024)(128)(4,1)} %bitcast.17), calls=%async_computation.6 | async-start | bytes 2097152
Sparse Core Ops, SparseCore 0:
  969.4 174.8 all-gather.2
where the time goes:
time: 1270 us; the launch traced here: 1260 us
  blocking collectives  815 us (64%)
  local copies, waits for them, and re-layouts  228 us (18%)
  waiting for transfers between devices  125 us (10%)
  other arithmetic  81 us (6%)
  between operations  15.7 us (1%)
    all_to_all x1, blocking collectives, body(): lax.all_to_all(lax.all_to_all(blocks[None], 'grp', split_axis=1, concat_a...  414 us
    all_to_all x1, blocking collectives, body(): lax.all_to_all(blocks[None], 'grp', split_axis=1, concat_axis=0, tiled=True)  219 us
    unnamed x10, local copies, waits for them, and re-layouts  154 us
    all_to_all x1, blocking collectives, body(): lax.all_to_all(fresh, 'zero', split_axis=4, concat_axis=1, tiled=True)  145 us
    all_gather x1, waiting for transfers between devices, body(): tiled = lax.all_gather(own_tiles, 'grp', axis=0, tiled=True)  125 us
    psum x1, blocking collectives, body(): total = lax.psum(jnp.sum(summed * summed), ('grp', 'zero'))  38.2 us
    reshape x1, other arithmetic, body(): new_master.astype(jnp.bfloat16).reshape(1, 1, rows_dev, 2, full_width)  33.4 us
  transfers between devices with their start and end apart: 1, of which 1 were waited for; matrix products, arithmetic and copies ran while one was open for 4% of the time, Pallas kernels for 0%

commit v1 on v0

--- a/solution.py
+++ b/solution.py
@@ -45,7 +45,9 @@
         summed, master_weights, first_moment, second_moment, scale
     )
     fresh = new_master.astype(jnp.bfloat16).reshape(1, 1, rows_dev, 2, full_width)
-    own_tiles = lax.all_to_all(fresh, "zero", split_axis=4, concat_axis=1, tiled=True)
+    pieces = jnp.split(fresh, lax.axis_size("zero"), axis=4)
+    arrived_2 = lax.all_to_all(jnp.stack(pieces), "zero", 0, 0)
+    own_tiles = jnp.concatenate(arrived_2, axis=1)
     tiled = lax.all_gather(own_tiles, "grp", axis=0, tiled=True)
     new_weights = tiled.reshape(groups * shards * rows_dev, 2, full_width // shards)
     return (new_master, new_first, new_second, new_weights)

time: 1270 us -> 1200 us (0.945)
  blocking collectives: 815 us -> 780 us
  local copies, waits for them, and re-layouts: 228 us -> 198 us
    all_to_all x1, blocking collectives: 145 us -> 109 us  [body(): arrived_2 = lax.all_to_all(jnp.stack(pieces), 'zero', 0, 0)]
    all_to_all x1 -> x0, local copies, waits for them, and re-layouts: 15.8 us -> none  [body(): lax.all_to_all(fresh, 'zero', split_axis=4, concat_axis=1, tiled=True)]
    reshape x1 -> x0, local copies, waits for them, and re-layouts: 14.1 us -> none  [body(): new_master.astype(jnp.bfloat16).reshape(1, 1, rows_dev, 2, full_width)]
    unnamed x10 -> x17, local copies, waits for them, and re-layouts: 154 us -> 154 us
where the time goes in v1:
time: 1200 us
  blocking collectives  780 us (65%)
  local copies, waits for them, and re-layouts  198 us (16%)
  waiting for transfers between devices  125 us (10%)
  other arithmetic  79.7 us (7%)
  between operations  15.8 us (1%)
    all_to_all x1, blocking collectives, body(): lax.all_to_all(lax.all_to_all(blocks[None], 'grp', split_axis=1, concat_a...  414 us
    all_to_all x1, blocking collectives, body(): lax.all_to_all(blocks[None], 'grp', split_axis=1, concat_axis=0, tiled=True)  219 us
    unnamed x17, local copies, waits for them, and re-layouts  154 us
    all_gather x1, waiting for transfers between devices, body(): tiled = lax.all_gather(own_tiles, 'grp', axis=0, tiled=True)  125 us
    all_to_all x1, blocking collectives, body(): arrived_2 = lax.all_to_all(jnp.stack(pieces), 'zero', 0, 0)  109 us
    psum x1, blocking collectives, body(): total = lax.psum(jnp.sum(summed * summed), ('grp', 'zero'))  38.2 us
    reshape x1, other arithmetic, body(): new_master.astype(jnp.bfloat16).reshape(1, 1, rows_dev, 2, full_width)  32.1 us
  transfers between devices with their start and end apart: 1, of which 1 were waited for; matrix products, arithmetic and copies ran while one was open for 4% of the time, Pallas kernels for 0%

profile of v1, /device:TPU:0, one launch (start us, length us, event | category | flops | bytes accessed | tf_op | source)
XLA Modules:
  0.0 1198.1 jit_solution(150609943634955342)
XLA Ops:
  7.2 0.0 all-gather.3.cloned.1.call-start
  7.2 218.8 %all_to_all.26 = bf16[1,4,8,96,2,1536]{5,4,3,2,0,1:T(2,128)(2,1)} all-to-all(bf16[1,4,8,96,2,1536]{5,4,3,2,0,1:T(2,128)(2,1)} %bitcast.49), channel_id=1, replica_groups=mesh['grp'=4,'zero'=8] {'grp'}, dimensions={1} | all-to-all | bytes 37748736 | tf_op jit(solution)/shard_map/all_to_all | solution.py:34
  226.0 15.4 %copy.29 = bf16[4,1,8,96,2,1536]{5,4,3,0,1,2:T(2,128)(2,1)S(1)} copy(bf16[4,1,8,96,2,1536]{5,4,3,2,0,1:T(2,128)(2,1)} %bitcast.46) | data formatting | bytes 37748736 | tf_op jit(solution)/shard_map/all_to_all | solution.py:34
  241.4 413.5 %all_to_all.27 = bf16[4,1,8,96,2,1536]{5,4,3,0,1,2:T(2,128)(2,1)} all-to-all(bf16[4,1,8,96,2,1536]{5,4,3,0,1,2:T(2,128)(2,1)S(1)} %copy.29), channel_id=1, replica_groups=mesh['grp'=4,'zero'=8] {'zero'}, dimensions={2} | all-to-all | bytes 37748736 | tf_op jit(solution)/shard_map/all_to_all | solution.py:33
  654.9 17.5 %convert_reduce_fusion = f32[8,96,2,1536]{3,1,2,0:T(8,128)} fusion(bf16[4,1,8,96,2,1536]{5,4,3,0,1,2:T(2,128)(2,1)} %all_to_all.27), kind=kLoop, calls=%fused_computation | loop fusion | flops 16515072 | bytes 28311552 | tf_op jit(solution)/shard_map/reduce_sum | solution.py:40
  672.5 14.0 %multiply_reduce_fusion = f32[]{:T(128)} fusion(f32[8,96,2,1536]{3,1,2,0:T(8,128)} %convert_reduce_fusion), kind=kLoop, calls=%fused_computation.8 | loop fusion | flops 4718591 | bytes 9437188 | tf_op jit(solution)/shard_map/reduce_sum | solution.py:42
  687.1 38.2 %psum.7 = f32[]{:T(128)} all-reduce(f32[]{:T(128)} %multiply_reduce_fusion), channel_id=1, replica_groups=mesh['grp'=4,'zero'=8] {'grp','zero'}, use_global_device_ids=true, to_apply=%region_2.0 | all-reduce | flops 1 | bytes 8 | tf_op jit(solution)/shard_map/psum | solution.py:42
  726.0 16.1 %multiply_bitcast_fusion = f32[96,2,8,1536]{3,1,0,2:T(2,128)S(1)} fusion(f32[8,96,2,1536]{3,1,2,0:T(8,128)} %convert_reduce_fusion, f32[]{:T(128)S(6)} %min_shard_map.3), kind=kLoop, calls=%fused_computation.7 | loop fusion | flops 2359296 | bytes 18874372 | tf_op jit(solution)/shard_map/mul | solution.py:15
  742.1 9.2 copy.32
  751.3 10.0 mul.56
  761.3 32.1 %convert_bitcast_fusion = (bf16[1,1,96,2,12288]{4,2,3,1,0:T(8,128)(2,1)S(1)}, f32[96,2,12288]{2,0,1:T(8,128)}, f32[96,2,12288]{2,0,1:T(8,128)}, f32[96,2,12288]{2,0,1:T(8,128)}) fusion(f32[96,2,12288]{2,1,0:T(2,128)} %param.6, f32[96,2,12288]{2,0,1:T(8,128)} %mul.56, f32[96,2,12288]{2,1,0:T(2,128)} %param.7, f32[96,2,12288]{2,1,0:T(2,128)} %param.8), kind=kLoop, calls=%fused_computation.9 | loop fusion | flops 33030144 | bytes 70778880 | tf_op jit(solution)/shard_map/reshape | solution.py:47
  793.8 109.1 %all_to_all.28 = bf16[8,1,1,96,2,1536]{5,3,4,2,1,0:T(8,128)(2,1)} all-to-all(bf16[8,1,1,96,2,1536]{5,3,4,2,1,0:T(8,128)(2,1)S(1)} %fusion.2), channel_id=1, replica_groups=mesh['grp'=4,'zero'=8] {'zero'}, dimensions={0} | all-to-all | bytes 9437184 | tf_op jit(solution)/shard_map/all_to_all | solution.py:49
  902.9 0.0 all-gather.3.cloned.1.call-update
  903.0 0.0 slice-start
  903.0 0.0 slice-start.1
  903.0 17.2 %copy.36 = f32[96,2,12288]{2,1,0:T(2,128)} copy(f32[96,2,12288]{2,0,1:T(8,128)} %get-tuple-element.17) | data formatting | bytes 18874368
  920.2 0.0 slice-start.2
  920.2 17.1 %copy.37 = f32[96,2,12288]{2,1,0:T(2,128)} copy(f32[96,2,12288]{2,0,1:T(8,128)} %get-tuple-element.18) | data formatting | bytes 18874368
  937.3 0.0 slice-done
  937.3 0.0 slice-done.1
  937.3 0.0 slice-done.2
  937.4 16.1 %copy.38 = f32[96,2,12288]{2,1,0:T(2,128)} copy(f32[96,2,12288]{2,0,1:T(8,128)S(1)} %bitcast.48) | data formatting | bytes 18874368
  953.5 124.7 %all-gather.3.cloned.1.call-done = bf16[32,1,1,96,2,1536]{5,3,4,2,1,0:T(8,128)(2,1)} async-done(((bf16[8,1,1,96,2,1536]{5,3,4,2,1,0:T(8,128)(2,1)}), bf16[32,1,1,96,2,1536]{5,3,4,2,1,0:T(8,128)(2,1)}) %all-gather.3.cloned.1.call-update) | async-done | bytes 18874384 | tf_op jit(solution)/shard_map/all_gather | solution.py:51
  1078.1 9.5 copy.35
  1087.6 103.4 %copy.39 = bf16[3072,2,1536]{2,1,0:T(2,128)(2,1)} copy(bf16[3072,2,1536]{2,0,1:T(8,128)(2,1)S(1)} %bitcast.45) | data formatting | bytes 37748736
  (9 shorter events, 0.3 us)
Async XLA Ops:
  7.2 1071.0 %all-gather.3.cloned.1.call-start = ((), (), s32[]{:S(2)}) async-start(), calls=%async_computation.3 | async-start | bytes 23592960 | tf_op jit(solution)/shard_map/all_gather | solution.py:51
  903.0 34.4 %slice-start = ((s8[9437184]{0:T(1024)(128)(4,1)}), s8[4194304]{0:T(1024)(128)(4,1)S(1)}, s32[]{:S(2)}) async-start(s8[9437184]{0:T(1024)(128)(4,1)} %bitcast.47), calls=%async_computation.4 | async-start | bytes 8388608
  903.0 34.4 %slice-start.1 = ((s8[9437184]{0:T(1024)(128)(4,1)}), s8[4194304]{0:T(1024)(128)(4,1)S(1)}, s32[]{:S(2)}) async-start(s8[9437184]{0:T(1024)(128)(4,1)} %bitcast.47), calls=%async_computation.5 | async-start | bytes 8388608
  920.2 17.2 %slice-start.2 = ((s8[9437184]{0:T(1024)(128)(4,1)}), s8[1048576]{0:T(1024)(128)(4,1)S(1)}, s32[]{:S(2)}) async-start(s8[9437184]{0:T(1024)(128)(4,1)} %bitcast.47), calls=%async_computation.6 | async-start | bytes 2097152
Sparse Core Ops, SparseCore 0:
  903.1 174.9 all-gather.2
